TPU v7x, 128 devices: a whole 4x4x4 slice. The times are simulated.
128 devices in a mesh: tm: 16 (over z, y), space: 8 (over x, core).
Axes of the slice: x: 4, y: 4, z: 4, core: 2. Of those that a mesh axis runs over, the one named last changes fastest.
Arguments:
- initial_guess: float32 [16, 1024, 1024], P('tm', 'space'), may hold values from -6 to 6
- start_field: float32 [1024, 1024], P('space'), may hold values from -6 to 6
- source_field: float32 [1024, 1024], P('space'), may hold values from -0.3 to 0.3
Outputs:
- final_states: float32 [16, 1024, 1024], P('tm', 'space')
All inputs are finite; a program needn't handle non-finite values.
Results may differ from a plain program's by a relative error of at most 0.00013.
Values sent between devices are 32-bit elements; how exact they have to be, the bound alone decides.
No kernel may reach another device: no remote copies, remote signals or barrier semaphores. Data moves between devices by JAX's collectives and lax.ppermute only.
A program may use at most 64 MiB of HBM per device.

v0:
```python
import functools

import jax
import jax.numpy as jnp
import ml_dtypes
import numpy as np
from jax import lax
from jax.experimental import pallas as pl
from jax.experimental.pallas import tpu as pltpu
from jax.sharding import PartitionSpec as P

M = 16
RADIX = 8
RESIDUES = (0, 4, 1, 7, 2, 6, 3, 5)
AXES = ("tm", "space")

decay_rate = 0.0005
spread_rate = 0.01


def kernel_matrices(length):
    width = length // RADIX
    cells = np.arange(width)

    def cas(modes, sign):
        angles = 2.0 * np.pi / length * (cells[:, None] * modes[None, :] % length)
        return np.cos(angles) + sign * np.sin(angles)

    def modes(residue):
        return residue + RADIX * np.arange(width)

    zero = np.zeros((width, width))
    matrices = [np.block([[cas(modes(0), 1), zero], [zero, cas(modes(4), 1)]])]
    for q in (1, 2, 3):
        one, other = modes(q), modes(RADIX - q)
        matrices.append(np.block([[cas(one, 1), cas(other, 1)], [cas(one, -1), -cas(other, -1)]]))
    full = np.stack(matrices).astype(np.float32)
    high = full.astype(ml_dtypes.bfloat16)
    low = (full - high.astype(np.float32)).astype(ml_dtypes.bfloat16)
    return high, low


def product(value, high, low, contract):
    value_high = value.astype(jnp.bfloat16)
    value_low = (value - value_high.astype(jnp.float32)).astype(jnp.bfloat16)
    dims = (((1,), (contract,)), ((), ()))
    dot = functools.partial(lax.dot_general, dimension_numbers=dims, preferred_element_type=jnp.float32)
    return dot(value_high, high) + (dot(value_low, high) + dot(value_high, low))


def to_modes(v, high, low):
    root = float(np.sqrt(0.5))
    s = [v[b] + v[b + 4] for b in range(4)]
    d = [v[b] - v[b + 4] for b in range(4)]
    even, odd = s[0] + s[2], s[1] + s[3]
    near, far = root * (d[1] - d[3]), root * (d[1] + d[3])
    pairs = (
        (even + odd, even - odd),
        (d[0] + near, far + d[2]),
        (s[0] - s[2], s[1] - s[3]),
        (d[0] - near, far - d[2]),
    )
    return [product(jnp.concatenate(pair, axis=1), high[i], low[i], 0) for i, pair in enumerate(pairs)]


def to_cells(h, high, low):
    root = float(np.sqrt(0.5))
    width = h[0].shape[1] // 2
    pairs = [product(h[i], high[i], low[i], 1) for i in range(4)]
    (a0, a4), (a1, b1), (a2, b2), (a3, b3) = [(pair[:, :width], pair[:, width:]) for pair in pairs]
    e, g = a0 + a4, a0 - a4
    p, m, q, n = a1 + a3, a1 - a3, b1 + b3, b1 - b3
    ep, em, gp, gm = e + a2, e - a2, g + b2, g - b2
    up, down = root * (m + q), root * (q - m)
    return [ep + p, gp + up, em + n, gm + down, ep - p, gp - up, em - n, gm - down]


def columns_forward(guess_ref, start_ref, source_ref, high_ref, low_ref, out_ref, field, copied):
    last = lax.axis_size("tm") - 1
    place = lax.axis_index("tm")

    def fetch(ref):
        copy = pltpu.make_async_copy(ref, field, copied)
        copy.start()
        copy.wait()

    @pl.when(place < last - 1)
    def _():
        fetch(guess_ref.at[0])

    @pl.when(place == last - 1)
    def _():
        fetch(start_ref)

    @pl.when(place == last)
    def _():
        fetch(source_ref)

    width = field.shape[1] // RADIX
    v = [field[:, b * width : (b + 1) * width] for b in range(RADIX)]
    h = to_modes(v, high_ref, low_ref)
    for i in range(4):
        out_ref[2 * width * i : 2 * width * (i + 1), :] = h[i].T


def rows_and_time(in_ref, high_ref, low_ref, out_ref):
    times, blocks, group, width = in_ref.shape
    length = blocks * width
    rows = times * group
    v = [in_ref[:, b].reshape(rows, width) for b in range(blocks)]
    h = to_modes(v, high_ref, low_ref)

    device = lax.axis_index("tm") * lax.axis_size("space") + lax.axis_index("space")
    groups = width // group
    residue = jnp.int32(0)
    for i, q in enumerate(RESIDUES):
        residue = jnp.where(device // groups == i, q, residue)
    within = lax.rem(device, groups) * group
    sublane = lax.broadcasted_iota(jnp.int32, (group, 2 * width), 0)
    lane = lax.broadcasted_iota(jnp.int32, (group, 2 * width), 1)
    column_modes = residue + RADIX * (within + sublane)

    def half_sines(modes):
        return jnp.sin(jnp.pi / length * modes.astype(jnp.float32)) ** 2

    column_sines = half_sines(column_modes)
    outs = []
    for i in range(4):
        first, second = RESIDUES[2 * i], RESIDUES[2 * i + 1]
        row_modes = jnp.where(lane < width, first + RADIX * lane, second + RADIX * (lane - width))
        stiffness = 4.0 * (half_sines(row_modes) + column_sines)
        fine = 1.0 / (1.0 + decay_rate + spread_rate * stiffness)
        coarse = 1.0 / (1.0 + M * decay_rate + M * spread_rate * stiffness)
        power, forcing_symbol = fine, fine
        for _ in range(M - 1):
            power = power * fine
            forcing_symbol = forcing_symbol + power
        scale = 1.0 / (length * length)
        scaled_power = scale * power
        part = [h[i][t * group : (t + 1) * group] for t in range(times)]
        forcing = scale * forcing_symbol * part[times - 1]
        relaxed = scaled_power * part[times - 2] + forcing
        state = relaxed
        states = [state]
        gap = power - coarse
        for j in range(1, times):
            state = coarse * state + (gap * relaxed + forcing)
            states.append(state)
            if j < times - 1:
                relaxed = scaled_power * part[j - 1] + forcing
        outs.append(jnp.concatenate(states, axis=0))

    cells = to_cells(outs, high_ref, low_ref)
    for b in range(blocks):
        out_ref[:, b] = cells[b].reshape(times, group, width)


def columns_inverse(in_ref, high_ref, low_ref, out_ref):
    width = in_ref.shape[1]
    h = [in_ref[2 * width * i : 2 * width * (i + 1), :].T for i in range(4)]
    cells = to_cells(h, high_ref, low_ref)
    for b in range(RADIX):
        out_ref[0, :, b * width : (b + 1) * width] = cells[b]


def on_chip(count):
    return [pl.BlockSpec(memory_space=pltpu.VMEM)] * count


def anywhere(count):
    return [pl.BlockSpec(memory_space=pl.ANY)] * count


def body(initial_guess, start_field, source_field):
    rows, length = start_field.shape
    times, blocks = lax.axis_size("tm"), lax.axis_size("space")
    devices = times * blocks
    group = length // devices
    high, low = (jnp.asarray(part) for part in kernel_matrices(length))

    spectra = pl.pallas_call(
        columns_forward,
        out_shape=jax.ShapeDtypeStruct((length, rows), jnp.float32),
        in_specs=anywhere(3) + on_chip(2),
        out_specs=on_chip(1)[0],
        scratch_shapes=[pltpu.VMEM((rows, length), jnp.float32), pltpu.SemaphoreType.DMA],
        name="columns_forward",
    )(initial_guess, start_field, source_field, high, low)

    spectra = spectra.reshape(devices, group, rows)
    spectra = lax.all_to_all(spectra, AXES, split_axis=0, concat_axis=0, tiled=True)
    states = pl.pallas_call(
        rows_and_time,
        out_shape=jax.ShapeDtypeStruct((times, blocks, group, rows), jnp.float32),
        in_specs=on_chip(3),
        out_specs=on_chip(1)[0],
        name="rows_and_time",
    )(spectra.reshape(times, blocks, group, rows), high, low)

    states = states.reshape(devices, group, rows)
    states = lax.all_to_all(states, AXES, split_axis=0, concat_axis=0, tiled=True)
    return pl.pallas_call(
        columns_inverse,
        out_shape=jax.ShapeDtypeStruct((1, rows, length), jnp.float32),
        in_specs=on_chip(3),
        out_specs=on_chip(1)[0],
        name="columns_inverse",
    )(states.reshape(length, rows), high, low)


def solution(mesh):
    in_specs = (P("tm", "space", None), P("space", None), P("space", None))
    out_specs = P("tm", "space", None)
    return jax.shard_map(body, mesh=mesh, in_specs=in_specs, out_specs=out_specs, check_vma=False)
```

profile of v0, /device:TPU:1, one launch (start us, length us, event | category | flops | bytes accessed | tf_op | source)
XLA Modules:
  0.0 53.7 jit_solution(6529522667596139808)
XLA Ops:
  0.0 3.5 %columns_forward.1 = f32[1024,128]{1,0:T(8,128)} custom-call(f32[1,128,1024]{2,1,0:T(8,128)} %guess_ref.1, f32[128,1024]{1,0:T(8,128)} %start_ref.1, f32[128,1024]{1,0:T(8,128)} %source_ref.1, bf16[4,256,256]{2,1,0:T(8,128)(2,1)} %constant.4.clone.high_ref, bf16[4,256,256]{2,1,0:T(8,128)(2,1)} %constant.5.clone.low_ref), custom_call_target="tpu_custom_call" | custom-call | tf_op jit(solution)/shard_map/columns_forward/pallas_call | solution.py:181
  3.5 25.2 %all_to_all.10 = f32[128,8,128]{2,1,0:T(8,128)} all-to-all(f32[128,8,128]{2,1,0:T(8,128)} %bitcast.7), channel_id=1, replica_groups=mesh['tm'=16,'space'=8] {'tm','space'}, dimensions={0} | all-to-all | bytes 1048576 | tf_op jit(solution)/shard_map/all_to_all | solution.py:191
  28.8 3.1 %rows_and_time.1 = f32[16,8,8,128]{3,2,1,0:T(8,128)} custom-call(f32[16,8,8,128]{3,2,1,0:T(8,128)} %bitcast.5, bf16[4,256,256]{2,1,0:T(8,128)(2,1)} %constant.4.clone.high_ref, bf16[4,256,256]{2,1,0:T(8,128)(2,1)} %constant.5.clone.low_ref), custom_call_target="tpu_custom_call" | custom-call | tf_op jit(solution)/shard_map/rows_and_time/pallas_call | solution.py:192
  31.9 19.0 %all_to_all.11 = f32[128,8,128]{2,1,0:T(8,128)} all-to-all(f32[128,8,128]{2,1,0:T(8,128)} %bitcast.6), channel_id=1, replica_groups=mesh['tm'=16,'space'=8] {'tm','space'}, dimensions={0} | all-to-all | bytes 1048576 | tf_op jit(solution)/shard_map/all_to_all | solution.py:201
  50.9 2.8 %columns_inverse.1 = f32[1,128,1024]{2,1,0:T(8,128)} custom-call(f32[1024,128]{1,0:T(8,128)} %bitcast.4, bf16[4,256,256]{2,1,0:T(8,128)(2,1)} %constant.4.clone.high_ref, bf16[4,256,256]{2,1,0:T(8,128)(2,1)} %constant.5.clone.low_ref), custom_call_target="tpu_custom_call" | custom-call | tf_op jit(solution)/shard_map/columns_inverse/pallas_call | solution.py:202
where the time goes:
time: 54 us; the launch traced here: 53.7 us
  blocking collectives  44.3 us (82%)
  Pallas kernels  9.38 us (17%)
    all_to_all x1, blocking collectives, body(): lax.all_to_all(spectra, AXES, split_axis=0, concat_axis=0, tiled=True)  25.2 us
    all_to_all x1, blocking collectives, body(): lax.all_to_all(states, AXES, split_axis=0, concat_axis=0, tiled=True)  19 us
    pallas_call x1, Pallas kernels, body(): pl.pallas_call(columns_forward, out_shape=jax.ShapeDtypeStruct((length, r...  3.53 us
    pallas_call x1, Pallas kernels, body(): pl.pallas_call(rows_and_time, out_shape=jax.ShapeDtypeStruct((times, bloc...  3.1 us
    pallas_call x1, Pallas kernels, body(): pl.pallas_call(columns_inverse, out_shape=jax.ShapeDtypeStruct((1, rows,...  2.75 us

commit v1 on v0

v1 whole, which is shorter than its diff:
```python
import functools

import jax
import jax.numpy as jnp
import ml_dtypes
import numpy as np
from jax import lax
from jax.experimental import pallas as pl
from jax.experimental.pallas import tpu as pltpu
from jax.sharding import Mesh
from jax.sharding import PartitionSpec as P

M = 16
RADIX = 8
RESIDUES = (0, 4, 1, 1, 2, 2, 3, 3)
AXES = ("core", "z", "y", "x")
TM, SPACE = ("z", "y"), ("x", "core")
LIMIT = pltpu.CompilerParams(vmem_limit_bytes=8 * 1024 * 1024)

decay_rate = 0.0005
spread_rate = 0.01


def kernel_matrices(length):
    width = length // RADIX
    cells = np.arange(width)

    def cas(residue, sign):
        modes = residue + RADIX * np.arange(width)
        angles = 2.0 * np.pi / length * (cells[:, None] * modes[None, :] % length)
        return np.cos(angles) + sign * np.sin(angles)

    blocks = [cas(0, 1), cas(4, 1)] + [cas(q, sign) for q in (1, 2, 3) for sign in (1, -1)]
    full = np.stack(blocks).astype(np.float32)
    high = full.astype(ml_dtypes.bfloat16)
    low = (full - high.astype(np.float32)).astype(ml_dtypes.bfloat16)
    return high, low


def matrix(blocks, i):
    one, other = blocks[2 * i], blocks[2 * i + 1]
    if i == 0:
        zero = jnp.zeros_like(one)
        rows = ((one, zero), (zero, other))
    else:
        rows = ((one, other), (other, -one))
    return jnp.concatenate([jnp.concatenate(row, axis=1) for row in rows], axis=0)


def product(value, high, low, i, contract):
    value_high = value.astype(jnp.bfloat16)
    value_low = (value - value_high.astype(jnp.float32)).astype(jnp.bfloat16)
    dims = (((1,), (contract,)), ((), ()))
    dot = functools.partial(lax.dot_general, dimension_numbers=dims, preferred_element_type=jnp.float32)
    matrix_high, matrix_low = matrix(high, i), matrix(low, i)
    return dot(value_high, matrix_high) + (dot(value_low, matrix_high) + dot(value_high, matrix_low))


def to_pairs(v):
    root = float(np.sqrt(0.5))
    s = [v[b] + v[b + 4] for b in range(4)]
    d = [v[b] - v[b + 4] for b in range(4)]
    even, odd = s[0] + s[2], s[1] + s[3]
    near, far = root * (d[1] - d[3]), root * (d[1] + d[3])
    pairs = (
        (even + odd, even - odd),
        (d[0] + near, far + d[2]),
        (s[0] - s[2], s[1] - s[3]),
        (d[0] - near, far - d[2]),
    )
    return [jnp.concatenate(pair, axis=1) for pair in pairs]


def to_modes(pairs, high, low):
    return [product(pair, high, low, i, 0) for i, pair in enumerate(pairs)]


def to_cells(h, high, low):
    root = float(np.sqrt(0.5))
    width = h[0].shape[1] // 2
    pairs = [product(h[i], high, low, i, 1) for i in range(4)]
    (a0, a4), (a1, b1), (a2, b2), (a3, b3) = [(pair[:, :width], pair[:, width:]) for pair in pairs]
    e, g = a0 + a4, a0 - a4
    p, m, q, n = a1 + a3, a1 - a3, b1 + b3, b1 - b3
    ep, em, gp, gm = e + a2, e - a2, g + b2, g - b2
    up, down = root * (m + q), root * (q - m)
    return [ep + p, gp + up, em + n, gm + down, ep - p, gp - up, em - n, gm - down]


def columns_forward(guess_ref, start_ref, source_ref, high_ref, low_ref, out_ref, field, high, low, copied):
    last = lax.axis_size("z") * lax.axis_size("y") - 1
    place = lax.axis_index("z") * lax.axis_size("y") + lax.axis_index("y")

    def fetch(ref):
        pltpu.make_async_copy(ref, field, copied.at[0]).start()

    @pl.when(place < last - 1)
    def _():
        fetch(guess_ref.at[0])

    @pl.when(place == last - 1)
    def _():
        fetch(start_ref)

    @pl.when(place == last)
    def _():
        fetch(source_ref)

    matrices = [
        pltpu.make_async_copy(high_ref, high, copied.at[1]),
        pltpu.make_async_copy(low_ref, low, copied.at[2]),
    ]
    for copy in matrices:
        copy.start()
    pltpu.make_async_copy(start_ref, field, copied.at[0]).wait()

    width = field.shape[1] // RADIX
    pairs = to_pairs([field[:, b * width : (b + 1) * width] for b in range(RADIX)])
    for copy in matrices:
        copy.wait()
    h = to_modes(pairs, high, low)
    for i in range(4):
        out_ref[2 * width * i : 2 * width * (i + 1), :] = h[i].T


def rows_and_time(in_ref, high_ref, low_ref, out_ref):
    cores, times, chips, group, width = in_ref.shape
    length = chips * cores * width
    rows = times * group
    v = [in_ref[b % cores, :, b // cores].reshape(rows, width) for b in range(chips * cores)]
    h = to_modes(to_pairs(v), high_ref, low_ref)

    device = 0
    for axis in AXES:
        device = device * lax.axis_size(axis) + lax.axis_index(axis)
    groups = width // group
    residue = jnp.int32(0)
    for i, q in enumerate(RESIDUES):
        residue = jnp.where(device // groups == i, q, residue)
    within = lax.rem(device, groups) * group
    sublane = lax.broadcasted_iota(jnp.int32, (group, width), 0)
    lane = lax.broadcasted_iota(jnp.int32, (group, width), 1)

    def half_sines(modes):
        return jnp.sin(jnp.pi / length * modes.astype(jnp.float32)) ** 2

    column_sines = half_sines(residue + RADIX * (within + sublane))

    def symbols(row_residue):
        stiffness = 4.0 * (half_sines(row_residue + RADIX * lane) + column_sines)
        fine = 1.0 / (1.0 + decay_rate + spread_rate * stiffness)
        coarse = 1.0 / (1.0 + M * decay_rate + M * spread_rate * stiffness)
        power, forcing_symbol = fine, fine
        for _ in range(M - 1):
            power = power * fine
            forcing_symbol = forcing_symbol + power
        return power, forcing_symbol, coarse

    known = {q: symbols(q) for q in sorted(set(RESIDUES))}
    outs = []
    for i in range(4):
        both = zip(known[RESIDUES[2 * i]], known[RESIDUES[2 * i + 1]])
        power, forcing_symbol, coarse = (jnp.concatenate(pair, axis=1) for pair in both)
        scale = 1.0 / (length * length)
        scaled_power = scale * power
        part = [h[i][t * group : (t + 1) * group] for t in range(times)]
        forcing = scale * forcing_symbol * part[times - 1]
        relaxed = scaled_power * part[times - 2] + forcing
        state = relaxed
        states = [state]
        gap = power - coarse
        for j in range(1, times):
            state = coarse * state + (gap * relaxed + forcing)
            states.append(state)
            if j < times - 1:
                relaxed = scaled_power * part[j - 1] + forcing
        outs.append(jnp.concatenate(states, axis=0))

    cells = to_cells(outs, high_ref, low_ref)
    for b in range(chips * cores):
        out_ref[b % cores, :, b // cores] = cells[b].reshape(times, group, width)


def columns_inverse(in_ref, high_ref, low_ref, out_ref):
    width = in_ref.shape[1]
    h = [in_ref[2 * width * i : 2 * width * (i + 1), :].T for i in range(4)]
    cells = to_cells(h, high_ref, low_ref)
    for b in range(RADIX):
        out_ref[0, :, b * width : (b + 1) * width] = cells[b]


def on_chip(count):
    return [pl.BlockSpec(memory_space=pltpu.VMEM)] * count


def off_chip(count):
    return [pl.BlockSpec(memory_space=pltpu.HBM)] * count


def body(initial_guess, start_field, source_field):
    rows, length = start_field.shape
    times, chips, cores = lax.axis_size(TM), lax.axis_size("x"), lax.axis_size("core")
    devices = times * chips * cores
    group = length // devices
    high, low = (jnp.asarray(part) for part in kernel_matrices(length))

    spectra = pl.pallas_call(
        columns_forward,
        out_shape=jax.ShapeDtypeStruct((length, rows), jnp.float32),
        in_specs=off_chip(5),
        out_specs=on_chip(1)[0],
        scratch_shapes=[
            pltpu.VMEM((rows, length), jnp.float32),
            pltpu.VMEM(high.shape, high.dtype),
            pltpu.VMEM(low.shape, low.dtype),
            pltpu.SemaphoreType.DMA((3,)),
        ],
        compiler_params=LIMIT,
        name="columns_forward",
    )(*(pltpu.with_memory_space_constraint(x, pltpu.HBM) for x in (initial_guess, start_field, source_field, high, low)))

    spectra = spectra.reshape(devices, group, rows)
    spectra = lax.all_to_all(spectra, AXES, split_axis=0, concat_axis=0, tiled=True)
    states = pl.pallas_call(
        rows_and_time,
        out_shape=jax.ShapeDtypeStruct((cores, times, chips, group, rows), jnp.float32),
        in_specs=on_chip(3),
        out_specs=on_chip(1)[0],
        compiler_params=LIMIT,
        name="rows_and_time",
    )(spectra.reshape(cores, times, chips, group, rows), high, low)

    states = states.reshape(devices, group, rows)
    states = lax.all_to_all(states, AXES, split_axis=0, concat_axis=0, tiled=True)
    return pl.pallas_call(
        columns_inverse,
        out_shape=jax.ShapeDtypeStruct((1, rows, length), jnp.float32),
        in_specs=on_chip(3),
        out_specs=on_chip(1)[0],
        compiler_params=LIMIT,
        name="columns_inverse",
    )(states.reshape(length, rows), high, low)


def solution(mesh):
    chips = mesh.shape["space"] // 2
    finer = Mesh(mesh.devices.reshape(4, -1, chips, 2), TM + SPACE)
    in_specs = (P(TM, SPACE, None), P(SPACE, None), P(SPACE, None))
    out_specs = P(TM, SPACE, None)
    return jax.shard_map(body, mesh=finer, in_specs=in_specs, out_specs=out_specs, check_vma=False)
```

time: 54 us -> 46.6 us (0.86)
  Pallas kernels: 9.38 us -> 4.04 us
  blocking collectives: 44.3 us -> 42.3 us
    pallas_call x1, Pallas kernels: 3.1 us -> 0.95 us  [body(): pl.pallas_call(rows_and_time, out_shape=jax.ShapeDtypeStruct((cores, time...]
    pallas_call x1, Pallas kernels: 3.53 us -> 1.7 us  [body(): pl.pallas_call(columns_forward, out_shape=jax.ShapeDtypeStruct((length, r...]
    all_to_all x1, blocking collectives: 19 us -> 17.5 us  [body(): lax.all_to_all(states, AXES, split_axis=0, concat_axis=0, tiled=True)]
    pallas_call x1, Pallas kernels: 2.75 us -> 1.39 us  [body(): pl.pallas_call(columns_inverse, out_shape=jax.ShapeDtypeStruct((1, rows,...]
where the time goes in v1:
time: 46.6 us; the launch traced here: 46.4 us
  blocking collectives  42.3 us (91%)
  Pallas kernels  4.04 us (9%)
    all_to_all x1, blocking collectives, body(): lax.all_to_all(spectra, AXES, split_axis=0, concat_axis=0, tiled=True)  24.8 us
    all_to_all x1, blocking collectives, body(): lax.all_to_all(states, AXES, split_axis=0, concat_axis=0, tiled=True)  17.5 us
    pallas_call x1, Pallas kernels, body(): pl.pallas_call(columns_forward, out_shape=jax.ShapeDtypeStruct((length, r...  1.7 us
    pallas_call x1, Pallas kernels, body(): pl.pallas_call(columns_inverse, out_shape=jax.ShapeDtypeStruct((1, rows,...  1.39 us
    pallas_call x1, Pallas kernels, body(): pl.pallas_call(rows_and_time, out_shape=jax.ShapeDtypeStruct((cores, time...  0.95 us

profile of v1, /device:TPU:1, one launch (start us, length us, event | category | flops | bytes accessed | tf_op | source)
XLA Modules:
  0.0 46.4 jit_solution(7097724335738691624)
XLA Ops:
  0.0 1.7 %columns_forward.1 = f32[1024,128]{1,0:T(8,128)S(1)} custom-call(f32[1,128,1024]{2,1,0:T(8,128)} %guess_ref.1, f32[128,1024]{1,0:T(8,128)} %start_ref.1, f32[128,1024]{1,0:T(8,128)} %source_ref.1, bf16[8,128,128]{2,1,0:T(8,128)(2,1)} %constant.4.clone.high_ref, bf16[8,128,128]{2,1,0:T(8,128)(2,1)} %constant.5.clone.low_ref), custom_call_target="tpu_custom_call" | custom-call | tf_op jit(solution)/shard_map/columns_forward/pallas_call | solution.py:207
  1.7 0.0 copy-start
  1.7 0.0 copy-start.1
  1.7 24.8 %all_to_all.10 = f32[128,8,128]{2,1,0:T(8,128)S(1)} all-to-all(f32[128,8,128]{2,1,0:T(8,128)S(1)} %bitcast.7), channel_id=1, replica_groups=mesh['z'=4,'y'=4,'x'=4,'core'=2] {'core','z','y','x'}, dimensions={0} | all-to-all | bytes 1048576 | tf_op jit(solution)/shard_map/all_to_all | solution.py:223
  26.5 0.0 copy-done
  26.5 0.0 copy-done.1
  26.5 0.9 %rows_and_time.1 = f32[2,16,4,8,128]{4,3,2,1,0:T(8,128)S(1)} custom-call(f32[2,16,4,8,128]{4,3,2,1,0:T(8,128)S(1)} %bitcast.5, bf16[8,128,128]{2,1,0:T(8,128)(2,1)S(1)} %copy-done.1, bf16[8,128,128]{2,1,0:T(8,128)(2,1)S(1)} %copy-done), custom_call_target="tpu_custom_call" | custom-call | tf_op jit(solution)/shard_map/rows_and_time/pallas_call | solution.py:224
  27.5 17.5 %all_to_all.11 = f32[128,8,128]{2,1,0:T(8,128)S(1)} all-to-all(f32[128,8,128]{2,1,0:T(8,128)S(1)} %bitcast.6), channel_id=1, replica_groups=mesh['z'=4,'y'=4,'x'=4,'core'=2] {'core','z','y','x'}, dimensions={0} | all-to-all | bytes 1048576 | tf_op jit(solution)/shard_map/all_to_all | solution.py:234
  45.0 1.4 %columns_inverse.1 = f32[1,128,1024]{2,1,0:T(8,128)} custom-call(f32[1024,128]{1,0:T(8,128)S(1)} %bitcast.4, bf16[8,128,128]{2,1,0:T(8,128)(2,1)S(1)} %copy-done.1, bf16[8,128,128]{2,1,0:T(8,128)(2,1)S(1)} %copy-done), custom_call_target="tpu_custom_call" | custom-call | tf_op jit(solution)/shard_map/columns_inverse/pallas_call | solution.py:235
Async XLA Ops:
  1.7 24.8 %copy-start = (bf16[8,128,128]{2,1,0:T(8,128)(2,1)S(1)}, bf16[8,128,128]{2,1,0:T(8,128)(2,1)}, u32[]{:S(2)}) copy-start(bf16[8,128,128]{2,1,0:T(8,128)(2,1)} %constant.5.clone.low_ref) | copy-start | bytes 786436
  1.7 24.8 %copy-start.1 = (bf16[8,128,128]{2,1,0:T(8,128)(2,1)S(1)}, bf16[8,128,128]{2,1,0:T(8,128)(2,1)}, u32[]{:S(2)}) copy-start(bf16[8,128,128]{2,1,0:T(8,128)(2,1)} %constant.4.clone.high_ref) | copy-start | bytes 786436

commit v2 on v1

--- a/solution.py
+++ b/solution.py
@@ -1,5 +1,3 @@
-import functools
-
 import jax
 import jax.numpy as jnp
 import ml_dtypes
@@ -13,7 +11,7 @@
 M = 16
 RADIX = 8
 RESIDUES = (0, 4, 1, 1, 2, 2, 3, 3)
-AXES = ("core", "z", "y", "x")
+AXES = ("core", "z", "x", "y")
 TM, SPACE = ("z", "y"), ("x", "core")
 LIMIT = pltpu.CompilerParams(vmem_limit_bytes=8 * 1024 * 1024)
 
@@ -47,13 +45,26 @@
     return jnp.concatenate([jnp.concatenate(row, axis=1) for row in rows], axis=0)
 
 
-def product(value, high, low, i, contract):
-    value_high = value.astype(jnp.bfloat16)
-    value_low = (value - value_high.astype(jnp.float32)).astype(jnp.bfloat16)
-    dims = (((1,), (contract,)), ((), ()))
-    dot = functools.partial(lax.dot_general, dimension_numbers=dims, preferred_element_type=jnp.float32)
-    matrix_high, matrix_low = matrix(high, i), matrix(low, i)
-    return dot(value_high, matrix_high) + (dot(value_low, matrix_high) + dot(value_high, matrix_low))
+def split(value):
+    high = value.astype(jnp.bfloat16)
+    low = (value - high.astype(jnp.float32)).astype(jnp.bfloat16)
+    return jnp.concatenate([high, low], axis=0)
+
+
+def product(value, high, low, i):
+    count = value.shape[0]
+    parts = split(value)
+    twice = jnp.dot(parts, matrix(high, i), preferred_element_type=jnp.float32)
+    once = jnp.dot(parts[:count], matrix(low, i), preferred_element_type=jnp.float32)
+    return twice[:count] + (twice[count:] + once)
+
+
+def product_across(value, high, low, i):
+    count, modes = value.shape
+    matrices = jnp.concatenate([matrix(high, i), matrix(low, i)], axis=0)
+    dims = (((1,), (1,)), ((), ()))
+    both = lax.dot_general(matrices, split(value), dims, preferred_element_type=jnp.float32)
+    return both[:modes, :count] + (both[:modes, count:] + both[modes:, :count])
 
 
 def to_pairs(v):
@@ -72,13 +83,13 @@
 
 
 def to_modes(pairs, high, low):
-    return [product(pair, high, low, i, 0) for i, pair in enumerate(pairs)]
+    return [product(pair, high, low, i) for i, pair in enumerate(pairs)]
 
 
 def to_cells(h, high, low):
     root = float(np.sqrt(0.5))
     width = h[0].shape[1] // 2
-    pairs = [product(h[i], high, low, i, 1) for i in range(4)]
+    pairs = [product(h[i], high, low, i) for i in range(4)]
     (a0, a4), (a1, b1), (a2, b2), (a3, b3) = [(pair[:, :width], pair[:, width:]) for pair in pairs]
     e, g = a0 + a4, a0 - a4
     p, m, q, n = a1 + a3, a1 - a3, b1 + b3, b1 - b3
@@ -118,16 +129,22 @@
     pairs = to_pairs([field[:, b * width : (b + 1) * width] for b in range(RADIX)])
     for copy in matrices:
         copy.wait()
-    h = to_modes(pairs, high, low)
     for i in range(4):
-        out_ref[2 * width * i : 2 * width * (i + 1), :] = h[i].T
-
-
-def rows_and_time(in_ref, high_ref, low_ref, out_ref):
-    cores, times, chips, group, width = in_ref.shape
-    length = chips * cores * width
+        out_ref[2 * width * i : 2 * width * (i + 1), :] = product_across(pairs[i], high, low, i)
+
+
+def rows_and_time(in_ref, high_ref, low_ref, high_across_ref, low_across_ref, out_ref):
+    group, width = in_ref.shape[len(AXES) :]
+    sizes = dict(zip(AXES, in_ref.shape))
+    times, blocks = sizes["z"] * sizes["y"], sizes["x"] * sizes["core"]
+    length = blocks * width
     rows = times * group
-    v = [in_ref[b % cores, :, b // cores].reshape(rows, width) for b in range(chips * cores)]
+
+    def of_block(b):
+        place = {"x": b // sizes["core"], "core": b % sizes["core"]}
+        return tuple(place.get(axis, slice(None)) for axis in AXES)
+
+    v = [in_ref[of_block(b)].reshape(rows, width) for b in range(blocks)]
     h = to_modes(to_pairs(v), high_ref, low_ref)
 
     device = 0
@@ -176,9 +193,10 @@
                 relaxed = scaled_power * part[j - 1] + forcing
         outs.append(jnp.concatenate(states, axis=0))
 
-    cells = to_cells(outs, high_ref, low_ref)
-    for b in range(chips * cores):
-        out_ref[b % cores, :, b // cores] = cells[b].reshape(times, group, width)
+    cells = to_cells(outs, high_across_ref, low_across_ref)
+    for b in range(blocks):
+        place = of_block(b)
+        out_ref[place] = cells[b].reshape(sizes["z"], sizes["y"], group, width)
 
 
 def columns_inverse(in_ref, high_ref, low_ref, out_ref):
@@ -199,10 +217,12 @@
 
 def body(initial_guess, start_field, source_field):
     rows, length = start_field.shape
-    times, chips, cores = lax.axis_size(TM), lax.axis_size("x"), lax.axis_size("core")
-    devices = times * chips * cores
+    devices = lax.axis_size(AXES)
+    tiles = tuple(lax.axis_size(axis) for axis in AXES)
     group = length // devices
-    high, low = (jnp.asarray(part) for part in kernel_matrices(length))
+    matrices = kernel_matrices(length)
+    high, low = (jnp.asarray(part) for part in matrices)
+    high_across, low_across = (jnp.asarray(np.swapaxes(part, 1, 2)) for part in matrices)
 
     spectra = pl.pallas_call(
         columns_forward,
@@ -217,18 +237,18 @@
         ],
         compiler_params=LIMIT,
         name="columns_forward",
-    )(*(pltpu.with_memory_space_constraint(x, pltpu.HBM) for x in (initial_guess, start_field, source_field, high, low)))
+    )(*(pltpu.with_memory_space_constraint(x, pltpu.HBM) for x in (initial_guess, start_field, source_field, high_across, low_across)))
 
     spectra = spectra.reshape(devices, group, rows)
     spectra = lax.all_to_all(spectra, AXES, split_axis=0, concat_axis=0, tiled=True)
     states = pl.pallas_call(
         rows_and_time,
-        out_shape=jax.ShapeDtypeStruct((cores, times, chips, group, rows), jnp.float32),
-        in_specs=on_chip(3),
+        out_shape=jax.ShapeDtypeStruct(tiles + (group, rows), jnp.float32),
+        in_specs=on_chip(5),
         out_specs=on_chip(1)[0],
         compiler_params=LIMIT,
         name="rows_and_time",
-    )(spectra.reshape(cores, times, chips, group, rows), high, low)
+    )(spectra.reshape(tiles + (group, rows)), high, low, high_across, low_across)
 
     states = states.reshape(devices, group, rows)
     states = lax.all_to_all(states, AXES, split_axis=0, concat_axis=0, tiled=True)
@@ -239,7 +259,7 @@
         out_specs=on_chip(1)[0],
         compiler_params=LIMIT,
         name="columns_inverse",
-    )(states.reshape(length, rows), high, low)
+    )(states.reshape(length, rows), high_across, low_across)
 
 
 def solution(mesh):

time: 46.6 us -> 45.8 us (0.983)
  no operation moved by 1% of the time
where the time goes in v2:
time: 45.8 us; the launch traced here: 45.7 us
  blocking collectives  41.9 us (91%)
  Pallas kernels  3.65 us (8%)
    all_to_all x1, blocking collectives, body(): lax.all_to_all(spectra, AXES, split_axis=0, concat_axis=0, tiled=True)  24.4 us
    all_to_all x1, blocking collectives, body(): lax.all_to_all(states, AXES, split_axis=0, concat_axis=0, tiled=True)  17.5 us
    pallas_call x1, Pallas kernels, body(): pl.pallas_call(columns_forward, out_shape=jax.ShapeDtypeStruct((length, r...  1.68 us
    pallas_call x1, Pallas kernels, body(): pl.pallas_call(columns_inverse, out_shape=jax.ShapeDtypeStruct((1, rows,...  1.24 us

profile of v2, /device:TPU:1, one launch (start us, length us, event | category | flops | bytes accessed | tf_op | source)
XLA Modules:
  0.0 45.7 jit_solution(192682349690184131)
XLA Ops:
  0.0 1.7 %columns_forward.1 = f32[1024,128]{1,0:T(8,128)S(1)} custom-call(f32[1,128,1024]{2,1,0:T(8,128)} %guess_ref.1, f32[128,1024]{1,0:T(8,128)} %start_ref.1, f32[128,1024]{1,0:T(8,128)} %source_ref.1, bf16[8,128,128]{2,1,0:T(8,128)(2,1)} %constant.10.clone.high_ref.high_across_ref, bf16[8,128,128]{2,1,0:T(8,128)(2,1)} %constant.11.clone.low_ref.low_across_ref), custom_call_target="tpu_custom_call" | custom-call | tf_op jit(solution)/shard_map/columns_forward/pallas_call | solution.py:227
  1.7 0.0 copy-start
  1.7 0.0 copy-start.1
  1.7 0.0 copy-start.2
  1.7 0.0 copy-start.3
  1.7 24.4 %all_to_all.10 = f32[128,8,128]{2,1,0:T(8,128)S(1)} all-to-all(f32[128,8,128]{2,1,0:T(8,128)S(1)} %bitcast.5), channel_id=1, replica_groups=mesh['z'=4,'y'=4,'x'=4,'core'=2] {'core','z','x','y'}, dimensions={0} | all-to-all | bytes 1048576 | tf_op jit(solution)/shard_map/all_to_all | solution.py:243
  26.1 0.0 copy-done
  26.1 0.0 copy-done.1
  26.1 0.0 copy-done.2
  26.1 0.0 copy-done.3
  26.1 0.7 %rows_and_time.1 = f32[2,4,4,4,8,128]{5,4,3,2,1,0:T(8,128)S(1)} custom-call(f32[2,4,4,4,8,128]{5,4,3,2,1,0:T(8,128)S(1)} %bitcast.6, bf16[8,128,128]{2,1,0:T(8,128)(2,1)S(1)} %copy-done.3, bf16[8,128,128]{2,1,0:T(8,128)(2,1)S(1)} %copy-done.2, bf16[8,128,128]{2,1,0:T(8,128)(2,1)S(1)} %copy-done.1, bf16[8,128,128]{2,1,0:T(8,128)(2,1)S(1)} %copy-done), custom_call_target="tpu_custom_call" | custom-call | tf_op jit(solution)/shard_map/rows_and_time/pallas_call | solution.py:244
  26.9 17.5 %all_to_all.11 = f32[128,8,128]{2,1,0:T(8,128)S(1)} all-to-all(f32[128,8,128]{2,1,0:T(8,128)S(1)} %bitcast.7), channel_id=1, replica_groups=mesh['z'=4,'y'=4,'x'=4,'core'=2] {'core','z','x','y'}, dimensions={0} | all-to-all | bytes 1048576 | tf_op jit(solution)/shard_map/all_to_all | solution.py:254
  44.4 1.2 %columns_inverse.1 = f32[1,128,1024]{2,1,0:T(8,128)} custom-call(f32[1024,128]{1,0:T(8,128)S(1)} %bitcast.4, bf16[8,128,128]{2,1,0:T(8,128)(2,1)S(1)} %copy-done.1, bf16[8,128,128]{2,1,0:T(8,128)(2,1)S(1)} %copy-done), custom_call_target="tpu_custom_call" | custom-call | tf_op jit(solution)/shard_map/columns_inverse/pallas_call | solution.py:255
Async XLA Ops:
  1.7 24.4 %copy-start = (bf16[8,128,128]{2,1,0:T(8,128)(2,1)S(1)}, bf16[8,128,128]{2,1,0:T(8,128)(2,1)}, u32[]{:S(2)}) copy-start(bf16[8,128,128]{2,1,0:T(8,128)(2,1)} %constant.11.clone.low_ref.low_across_ref) | copy-start | bytes 786436
  1.7 24.4 %copy-start.1 = (bf16[8,128,128]{2,1,0:T(8,128)(2,1)S(1)}, bf16[8,128,128]{2,1,0:T(8,128)(2,1)}, u32[]{:S(2)}) copy-start(bf16[8,128,128]{2,1,0:T(8,128)(2,1)} %constant.10.clone.high_ref.high_across_ref) | copy-start | bytes 786436
  1.7 24.4 %copy-start.2 = (bf16[8,128,128]{2,1,0:T(8,128)(2,1)S(1)}, bf16[8,128,128]{2,1,0:T(8,128)(2,1)}, u32[]{:S(2)}) copy-start(bf16[8,128,128]{2,1,0:T(8,128)(2,1)} %constant.9.clone.low_ref) | copy-start | bytes 786436
  1.7 24.4 %copy-start.3 = (bf16[8,128,128]{2,1,0:T(8,128)(2,1)S(1)}, bf16[8,128,128]{2,1,0:T(8,128)(2,1)}, u32[]{:S(2)}) copy-start(bf16[8,128,128]{2,1,0:T(8,128)(2,1)} %constant.8.clone.high_ref) | copy-start | bytes 786436

commit v3 on v2

--- a/solution.py
+++ b/solution.py
@@ -65,6 +65,17 @@
     dims = (((1,), (1,)), ((), ()))
     both = lax.dot_general(matrices, split(value), dims, preferred_element_type=jnp.float32)
     return both[:modes, :count] + (both[:modes, count:] + both[modes:, :count])
+
+
+def product_down(value, high, low, i):
+    count = value.shape[1]
+    top = value.astype(jnp.bfloat16)
+    rest = (value - top.astype(jnp.float32)).astype(jnp.bfloat16)
+    parts = jnp.concatenate([top, rest], axis=1)
+    dims = (((0,), (0,)), ((), ()))
+    twice = lax.dot_general(parts, matrix(high, i), dims, preferred_element_type=jnp.float32)
+    once = lax.dot_general(top, matrix(low, i), dims, preferred_element_type=jnp.float32)
+    return twice[:count] + (twice[count:] + once)
 
 
 def to_pairs(v):
@@ -86,9 +97,9 @@
     return [product(pair, high, low, i) for i, pair in enumerate(pairs)]
 
 
-def to_cells(h, high, low):
+def to_cells(h, high, low, product=product):
     root = float(np.sqrt(0.5))
-    width = h[0].shape[1] // 2
+    width = high.shape[1]
     pairs = [product(h[i], high, low, i) for i in range(4)]
     (a0, a4), (a1, b1), (a2, b2), (a3, b3) = [(pair[:, :width], pair[:, width:]) for pair in pairs]
     e, g = a0 + a4, a0 - a4
@@ -98,55 +109,8 @@
     return [ep + p, gp + up, em + n, gm + down, ep - p, gp - up, em - n, gm - down]
 
 
-def columns_forward(guess_ref, start_ref, source_ref, high_ref, low_ref, out_ref, field, high, low, copied):
-    last = lax.axis_size("z") * lax.axis_size("y") - 1
-    place = lax.axis_index("z") * lax.axis_size("y") + lax.axis_index("y")
-
-    def fetch(ref):
-        pltpu.make_async_copy(ref, field, copied.at[0]).start()
-
-    @pl.when(place < last - 1)
-    def _():
-        fetch(guess_ref.at[0])
-
-    @pl.when(place == last - 1)
-    def _():
-        fetch(start_ref)
-
-    @pl.when(place == last)
-    def _():
-        fetch(source_ref)
-
-    matrices = [
-        pltpu.make_async_copy(high_ref, high, copied.at[1]),
-        pltpu.make_async_copy(low_ref, low, copied.at[2]),
-    ]
-    for copy in matrices:
-        copy.start()
-    pltpu.make_async_copy(start_ref, field, copied.at[0]).wait()
-
-    width = field.shape[1] // RADIX
-    pairs = to_pairs([field[:, b * width : (b + 1) * width] for b in range(RADIX)])
-    for copy in matrices:
-        copy.wait()
-    for i in range(4):
-        out_ref[2 * width * i : 2 * width * (i + 1), :] = product_across(pairs[i], high, low, i)
-
-
-def rows_and_time(in_ref, high_ref, low_ref, high_across_ref, low_across_ref, out_ref):
-    group, width = in_ref.shape[len(AXES) :]
-    sizes = dict(zip(AXES, in_ref.shape))
-    times, blocks = sizes["z"] * sizes["y"], sizes["x"] * sizes["core"]
-    length = blocks * width
-    rows = times * group
-
-    def of_block(b):
-        place = {"x": b // sizes["core"], "core": b % sizes["core"]}
-        return tuple(place.get(axis, slice(None)) for axis in AXES)
-
-    v = [in_ref[of_block(b)].reshape(rows, width) for b in range(blocks)]
-    h = to_modes(to_pairs(v), high_ref, low_ref)
-
+def write_symbols(out_ref, length):
+    residues, _, group, width = out_ref.shape
     device = 0
     for axis in AXES:
         device = device * lax.axis_size(axis) + lax.axis_index(axis)
@@ -162,22 +126,74 @@
         return jnp.sin(jnp.pi / length * modes.astype(jnp.float32)) ** 2
 
     column_sines = half_sines(residue + RADIX * (within + sublane))
-
-    def symbols(row_residue):
-        stiffness = 4.0 * (half_sines(row_residue + RADIX * lane) + column_sines)
+    for q in range(residues):
+        stiffness = 4.0 * (half_sines(q + RADIX * lane) + column_sines)
         fine = 1.0 / (1.0 + decay_rate + spread_rate * stiffness)
-        coarse = 1.0 / (1.0 + M * decay_rate + M * spread_rate * stiffness)
         power, forcing_symbol = fine, fine
         for _ in range(M - 1):
             power = power * fine
             forcing_symbol = forcing_symbol + power
-        return power, forcing_symbol, coarse
-
-    known = {q: symbols(q) for q in sorted(set(RESIDUES))}
+        out_ref[q, 0] = power
+        out_ref[q, 1] = forcing_symbol
+        out_ref[q, 2] = 1.0 / (1.0 + M * decay_rate + M * spread_rate * stiffness)
+
+
+def columns_forward(guess_ref, start_ref, source_ref, high_ref, low_ref, out_ref, symbols_ref, field, high, low, copied):
+    last = lax.axis_size("z") * lax.axis_size("y") - 1
+    place = lax.axis_index("z") * lax.axis_size("y") + lax.axis_index("y")
+
+    def fetch(ref):
+        pltpu.make_async_copy(ref, field, copied.at[0]).start()
+
+    @pl.when(place < last - 1)
+    def _():
+        fetch(guess_ref.at[0])
+
+    @pl.when(place == last - 1)
+    def _():
+        fetch(start_ref)
+
+    @pl.when(place == last)
+    def _():
+        fetch(source_ref)
+
+    matrices = [
+        pltpu.make_async_copy(high_ref, high, copied.at[1]),
+        pltpu.make_async_copy(low_ref, low, copied.at[2]),
+    ]
+    for copy in matrices:
+        copy.start()
+    write_symbols(symbols_ref, field.shape[1])
+    pltpu.make_async_copy(start_ref, field, copied.at[0]).wait()
+
+    width = field.shape[1] // RADIX
+    pairs = to_pairs([field[:, b * width : (b + 1) * width] for b in range(RADIX)])
+    for copy in matrices:
+        copy.wait()
+    for i in range(4):
+        out_ref[2 * width * i : 2 * width * (i + 1), :] = product_across(pairs[i], high, low, i)
+
+
+def rows_and_time(in_ref, symbols_ref, high_ref, low_ref, high_across_ref, low_across_ref, out_ref):
+    group, width = in_ref.shape[len(AXES) :]
+    sizes = dict(zip(AXES, in_ref.shape))
+    times, blocks = sizes["z"] * sizes["y"], sizes["x"] * sizes["core"]
+    length = blocks * width
+    rows = times * group
+
+    def of_block(b):
+        place = {"x": b // sizes["core"], "core": b % sizes["core"]}
+        return tuple(place.get(axis, slice(None)) for axis in AXES)
+
+    v = [in_ref[of_block(b)].reshape(rows, width) for b in range(blocks)]
+    h = to_modes(to_pairs(v), high_ref, low_ref)
+
     outs = []
     for i in range(4):
-        both = zip(known[RESIDUES[2 * i]], known[RESIDUES[2 * i + 1]])
-        power, forcing_symbol, coarse = (jnp.concatenate(pair, axis=1) for pair in both)
+        first, second = RESIDUES[2 * i], RESIDUES[2 * i + 1]
+        power, forcing_symbol, coarse = (
+            jnp.concatenate([symbols_ref[first, j], symbols_ref[second, j]], axis=1) for j in range(3)
+        )
         scale = 1.0 / (length * length)
         scaled_power = scale * power
         part = [h[i][t * group : (t + 1) * group] for t in range(times)]
@@ -201,8 +217,8 @@
 
 def columns_inverse(in_ref, high_ref, low_ref, out_ref):
     width = in_ref.shape[1]
-    h = [in_ref[2 * width * i : 2 * width * (i + 1), :].T for i in range(4)]
-    cells = to_cells(h, high_ref, low_ref)
+    h = [in_ref[2 * width * i : 2 * width * (i + 1), :] for i in range(4)]
+    cells = to_cells(h, high_ref, low_ref, product_down)
     for b in range(RADIX):
         out_ref[0, :, b * width : (b + 1) * width] = cells[b]
 
@@ -224,11 +240,12 @@
     high, low = (jnp.asarray(part) for part in matrices)
     high_across, low_across = (jnp.asarray(np.swapaxes(part, 1, 2)) for part in matrices)
 
-    spectra = pl.pallas_call(
+    symbols = (max(RESIDUES) + 1, 3, group, length // RADIX)
+    spectra, symbols = pl.pallas_call(
         columns_forward,
-        out_shape=jax.ShapeDtypeStruct((length, rows), jnp.float32),
+        out_shape=[jax.ShapeDtypeStruct(shape, jnp.float32) for shape in ((length, rows), symbols)],
         in_specs=off_chip(5),
-        out_specs=on_chip(1)[0],
+        out_specs=on_chip(2),
         scratch_shapes=[
             pltpu.VMEM((rows, length), jnp.float32),
             pltpu.VMEM(high.shape, high.dtype),
@@ -244,11 +261,11 @@
     states = pl.pallas_call(
         rows_and_time,
         out_shape=jax.ShapeDtypeStruct(tiles + (group, rows), jnp.float32),
-        in_specs=on_chip(5),
+        in_specs=on_chip(6),
         out_specs=on_chip(1)[0],
         compiler_params=LIMIT,
         name="rows_and_time",
-    )(spectra.reshape(tiles + (group, rows)), high, low, high_across, low_across)
+    )(spectra.reshape(tiles + (group, rows)), symbols, high, low, high_across, low_across)
 
     states = states.reshape(devices, group, rows)
     states = lax.all_to_all(states, AXES, split_axis=0, concat_axis=0, tiled=True)

time: 45.8 us -> 45.8 us (level)
  no operation moved by 1% of the time
where the time goes in v3:
time: 45.8 us; the launch traced here: 45.6 us
  blocking collectives  41.9 us (91%)
  Pallas kernels  3.61 us (8%)
    all_to_all x1, blocking collectives, body(): lax.all_to_all(spectra, AXES, split_axis=0, concat_axis=0, tiled=True)  24.4 us
    all_to_all x1, blocking collectives, body(): lax.all_to_all(states, AXES, split_axis=0, concat_axis=0, tiled=True)  17.5 us
    pallas_call x1, Pallas kernels, body(): pl.pallas_call(columns_forward, out_shape=[jax.ShapeDtypeStruct(shape, jn...  1.7 us
    pallas_call x1, Pallas kernels, body(): pl.pallas_call(columns_inverse, out_shape=jax.ShapeDtypeStruct((1, rows,...  1.21 us

profile of v3, /device:TPU:1, one launch (start us, length us, event | category | flops | bytes accessed | tf_op | source)
XLA Modules:
  0.0 45.6 jit_solution(17735200770836241820)
XLA Ops:
  0.0 1.7 %columns_forward.1 = (f32[1024,128]{1,0:T(8,128)S(1)}, f32[5,3,8,128]{3,2,1,0:T(8,128)S(1)}) custom-call(f32[1,128,1024]{2,1,0:T(8,128)} %guess_ref.1, f32[128,1024]{1,0:T(8,128)} %start_ref.1, f32[128,1024]{1,0:T(8,128)} %source_ref.1, bf16[8,128,128]{2,1,0:T(8,128)(2,1)} %constant.10.clone.high_ref.high_across_ref, ...), custom_call_target="tpu_custom_call" | custom-call | tf_op jit(solution)/shard_map/columns_forward/pallas_call | solution.py:244
  1.7 0.0 copy-start
  1.7 0.0 copy-start.1
  1.7 0.0 copy-start.2
  1.8 0.0 copy-start.3
  1.8 24.4 %all_to_all.10 = f32[128,8,128]{2,1,0:T(8,128)S(1)} all-to-all(f32[128,8,128]{2,1,0:T(8,128)S(1)} %bitcast.7), channel_id=1, replica_groups=mesh['z'=4,'y'=4,'x'=4,'core'=2] {'core','z','x','y'}, dimensions={0} | all-to-all | bytes 1048576 | tf_op jit(solution)/shard_map/all_to_all | solution.py:260
  26.1 0.0 copy-done
  26.1 0.0 copy-done.1
  26.1 0.0 copy-done.2
  26.1 0.0 copy-done.3
  26.2 0.7 %rows_and_time.1 = f32[2,4,4,4,8,128]{5,4,3,2,1,0:T(8,128)S(1)} custom-call(f32[2,4,4,4,8,128]{5,4,3,2,1,0:T(8,128)S(1)} %bitcast.5, f32[5,3,8,128]{3,2,1,0:T(8,128)S(1)} %get-tuple-element.8.symbols_ref, bf16[8,128,128]{2,1,0:T(8,128)(2,1)S(1)} %copy-done.3, bf16[8,128,128]{2,1,0:T(8,128)(2,1)S(1)} %copy-done.2, bf16[8,128,128]{2,1,0:T(8,128)(2,1)S(1)} %copy-done.1, ...), custom_call_target="tpu_custom_call" | custom-call | tf_op jit(solution)/shard_map/rows_and_time/pallas_call | solution.py:261
  26.9 17.5 %all_to_all.11 = f32[128,8,128]{2,1,0:T(8,128)S(1)} all-to-all(f32[128,8,128]{2,1,0:T(8,128)S(1)} %bitcast.6), channel_id=1, replica_groups=mesh['z'=4,'y'=4,'x'=4,'core'=2] {'core','z','x','y'}, dimensions={0} | all-to-all | bytes 1048576 | tf_op jit(solution)/shard_map/all_to_all | solution.py:271
  44.4 1.2 %columns_inverse.1 = f32[1,128,1024]{2,1,0:T(8,128)} custom-call(f32[1024,128]{1,0:T(8,128)S(1)} %bitcast.4, bf16[8,128,128]{2,1,0:T(8,128)(2,1)S(1)} %copy-done.1, bf16[8,128,128]{2,1,0:T(8,128)(2,1)S(1)} %copy-done), custom_call_target="tpu_custom_call" | custom-call | tf_op jit(solution)/shard_map/columns_inverse/pallas_call | solution.py:272
Async XLA Ops:
  1.7 24.4 %copy-start = (bf16[8,128,128]{2,1,0:T(8,128)(2,1)S(1)}, bf16[8,128,128]{2,1,0:T(8,128)(2,1)}, u32[]{:S(2)}) copy-start(bf16[8,128,128]{2,1,0:T(8,128)(2,1)} %constant.11.clone.low_ref.low_across_ref) | copy-start | bytes 786436
  1.7 24.4 %copy-start.1 = (bf16[8,128,128]{2,1,0:T(8,128)(2,1)S(1)}, bf16[8,128,128]{2,1,0:T(8,128)(2,1)}, u32[]{:S(2)}) copy-start(bf16[8,128,128]{2,1,0:T(8,128)(2,1)} %constant.10.clone.high_ref.high_across_ref) | copy-start | bytes 786436
  1.7 24.4 %copy-start.2 = (bf16[8,128,128]{2,1,0:T(8,128)(2,1)S(1)}, bf16[8,128,128]{2,1,0:T(8,128)(2,1)}, u32[]{:S(2)}) copy-start(bf16[8,128,128]{2,1,0:T(8,128)(2,1)} %constant.9.clone.low_ref) | copy-start | bytes 786436
  1.8 24.4 %copy-start.3 = (bf16[8,128,128]{2,1,0:T(8,128)(2,1)S(1)}, bf16[8,128,128]{2,1,0:T(8,128)(2,1)}, u32[]{:S(2)}) copy-start(bf16[8,128,128]{2,1,0:T(8,128)(2,1)} %constant.8.clone.high_ref) | copy-start | bytes 786436

commit v4 on v3

--- a/solution.py
+++ b/solution.py
@@ -52,11 +52,19 @@
 
 
 def product(value, high, low, i):
-    count = value.shape[0]
+    count, modes = value.shape
     parts = split(value)
-    twice = jnp.dot(parts, matrix(high, i), preferred_element_type=jnp.float32)
-    once = jnp.dot(parts[:count], matrix(low, i), preferred_element_type=jnp.float32)
-    return twice[:count] + (twice[count:] + once)
+
+    def times(left, upper, lower):
+        twice = jnp.dot(left, upper, preferred_element_type=jnp.float32)
+        once = jnp.dot(left[:count], lower, preferred_element_type=jnp.float32)
+        return twice[:count] + (twice[count:] + once)
+
+    if i == 0:
+        half = modes // 2
+        sides = (times(parts[:, j * half : (j + 1) * half], high[j], low[j]) for j in range(2))
+        return jnp.concatenate(list(sides), axis=1)
+    return times(parts, matrix(high, i), matrix(low, i))
 
 
 def product_across(value, high, low, i):

time: 45.8 us -> 45.8 us (level)
  no operation moved by 1% of the time
where the time goes in v4:
time: 45.8 us; the launch traced here: 45.6 us
  blocking collectives  41.9 us (91%)
  Pallas kernels  3.61 us (8%)
    all_to_all x1, blocking collectives, body(): lax.all_to_all(spectra, AXES, split_axis=0, concat_axis=0, tiled=True)  24.4 us
    all_to_all x1, blocking collectives, body(): lax.all_to_all(states, AXES, split_axis=0, concat_axis=0, tiled=True)  17.5 us
    pallas_call x1, Pallas kernels, body(): pl.pallas_call(columns_forward, out_shape=[jax.ShapeDtypeStruct(shape, jn...  1.7 us
    pallas_call x1, Pallas kernels, body(): pl.pallas_call(columns_inverse, out_shape=jax.ShapeDtypeStruct((1, rows,...  1.21 us

profile of v4, /device:TPU:1, one launch (start us, length us, event | category | flops | bytes accessed | tf_op | source)
XLA Modules:
  0.0 45.6 jit_solution(13748009222001554930)
XLA Ops:
  0.0 1.7 %columns_forward.1 = (f32[1024,128]{1,0:T(8,128)S(1)}, f32[5,3,8,128]{3,2,1,0:T(8,128)S(1)}) custom-call(f32[1,128,1024]{2,1,0:T(8,128)} %guess_ref.1, f32[128,1024]{1,0:T(8,128)} %start_ref.1, f32[128,1024]{1,0:T(8,128)} %source_ref.1, bf16[8,128,128]{2,1,0:T(8,128)(2,1)} %constant.10.clone.high_ref.high_across_ref, ...), custom_call_target="tpu_custom_call" | custom-call | tf_op jit(solution)/shard_map/columns_forward/pallas_call | solution.py:252
  1.7 0.0 copy-start
  1.7 0.0 copy-start.1
  1.7 0.0 copy-start.2
  1.8 0.0 copy-start.3
  1.8 24.4 %all_to_all.10 = f32[128,8,128]{2,1,0:T(8,128)S(1)} all-to-all(f32[128,8,128]{2,1,0:T(8,128)S(1)} %bitcast.7), channel_id=1, replica_groups=mesh['z'=4,'y'=4,'x'=4,'core'=2] {'core','z','x','y'}, dimensions={0} | all-to-all | bytes 1048576 | tf_op jit(solution)/shard_map/all_to_all | solution.py:268
  26.1 0.0 copy-done
  26.1 0.0 copy-done.1
  26.1 0.0 copy-done.2
  26.1 0.0 copy-done.3
  26.2 0.7 %rows_and_time.1 = f32[2,4,4,4,8,128]{5,4,3,2,1,0:T(8,128)S(1)} custom-call(f32[2,4,4,4,8,128]{5,4,3,2,1,0:T(8,128)S(1)} %bitcast.5, f32[5,3,8,128]{3,2,1,0:T(8,128)S(1)} %get-tuple-element.8.symbols_ref, bf16[8,128,128]{2,1,0:T(8,128)(2,1)S(1)} %copy-done.3, bf16[8,128,128]{2,1,0:T(8,128)(2,1)S(1)} %copy-done.2, bf16[8,128,128]{2,1,0:T(8,128)(2,1)S(1)} %copy-done.1, ...), custom_call_target="tpu_custom_call" | custom-call | tf_op jit(solution)/shard_map/rows_and_time/pallas_call | solution.py:269
  26.9 17.5 %all_to_all.11 = f32[128,8,128]{2,1,0:T(8,128)S(1)} all-to-all(f32[128,8,128]{2,1,0:T(8,128)S(1)} %bitcast.6), channel_id=1, replica_groups=mesh['z'=4,'y'=4,'x'=4,'core'=2] {'core','z','x','y'}, dimensions={0} | all-to-all | bytes 1048576 | tf_op jit(solution)/shard_map/all_to_all | solution.py:279
  44.4 1.2 %columns_inverse.1 = f32[1,128,1024]{2,1,0:T(8,128)} custom-call(f32[1024,128]{1,0:T(8,128)S(1)} %bitcast.4, bf16[8,128,128]{2,1,0:T(8,128)(2,1)S(1)} %copy-done.1, bf16[8,128,128]{2,1,0:T(8,128)(2,1)S(1)} %copy-done), custom_call_target="tpu_custom_call" | custom-call | tf_op jit(solution)/shard_map/columns_inverse/pallas_call | solution.py:280
Async XLA Ops:
  1.7 24.4 %copy-start = (bf16[8,128,128]{2,1,0:T(8,128)(2,1)S(1)}, bf16[8,128,128]{2,1,0:T(8,128)(2,1)}, u32[]{:S(2)}) copy-start(bf16[8,128,128]{2,1,0:T(8,128)(2,1)} %constant.11.clone.low_ref.low_across_ref) | copy-start | bytes 786436
  1.7 24.4 %copy-start.1 = (bf16[8,128,128]{2,1,0:T(8,128)(2,1)S(1)}, bf16[8,128,128]{2,1,0:T(8,128)(2,1)}, u32[]{:S(2)}) copy-start(bf16[8,128,128]{2,1,0:T(8,128)(2,1)} %constant.10.clone.high_ref.high_across_ref) | copy-start | bytes 786436
  1.7 24.4 %copy-start.2 = (bf16[8,128,128]{2,1,0:T(8,128)(2,1)S(1)}, bf16[8,128,128]{2,1,0:T(8,128)(2,1)}, u32[]{:S(2)}) copy-start(bf16[8,128,128]{2,1,0:T(8,128)(2,1)} %constant.9.clone.low_ref) | copy-start | bytes 786436
  1.8 24.4 %copy-start.3 = (bf16[8,128,128]{2,1,0:T(8,128)(2,1)S(1)}, bf16[8,128,128]{2,1,0:T(8,128)(2,1)}, u32[]{:S(2)}) copy-start(bf16[8,128,128]{2,1,0:T(8,128)(2,1)} %constant.8.clone.high_ref) | copy-start | bytes 786436

commit v5 on v4

--- a/solution.py
+++ b/solution.py
@@ -69,10 +69,20 @@
 
 def product_across(value, high, low, i):
     count, modes = value.shape
-    matrices = jnp.concatenate([matrix(high, i), matrix(low, i)], axis=0)
+    parts = split(value)
     dims = (((1,), (1,)), ((), ()))
-    both = lax.dot_general(matrices, split(value), dims, preferred_element_type=jnp.float32)
-    return both[:modes, :count] + (both[:modes, count:] + both[modes:, :count])
+
+    def times(upper, lower, right):
+        modes = upper.shape[0]
+        matrices = jnp.concatenate([upper, lower], axis=0)
+        both = lax.dot_general(matrices, right, dims, preferred_element_type=jnp.float32)
+        return both[:modes, :count] + (both[:modes, count:] + both[modes:, :count])
+
+    if i == 0:
+        half = modes // 2
+        sides = (times(high[j], low[j], parts[:, j * half : (j + 1) * half]) for j in range(2))
+        return jnp.concatenate(list(sides), axis=0)
+    return times(matrix(high, i), matrix(low, i), parts)
 
 
 def product_down(value, high, low, i):

time: 45.8 us -> 45.7 us (level)
  no operation moved by 1% of the time
where the time goes in v5:
time: 45.7 us; the launch traced here: 45.6 us
  blocking collectives  41.9 us (92%)
  Pallas kernels  3.57 us (8%)
    all_to_all x1, blocking collectives, body(): lax.all_to_all(spectra, AXES, split_axis=0, concat_axis=0, tiled=True)  24.4 us
    all_to_all x1, blocking collectives, body(): lax.all_to_all(states, AXES, split_axis=0, concat_axis=0, tiled=True)  17.5 us
    pallas_call x1, Pallas kernels, body(): pl.pallas_call(columns_forward, out_shape=[jax.ShapeDtypeStruct(shape, jn...  1.66 us
    pallas_call x1, Pallas kernels, body(): pl.pallas_call(columns_inverse, out_shape=jax.ShapeDtypeStruct((1, rows,...  1.21 us

profile of v5, /device:TPU:1, one launch (start us, length us, event | category | flops | bytes accessed | tf_op | source)
XLA Modules:
  0.0 45.6 jit_solution(14116512071333627946)
XLA Ops:
  0.0 1.7 %columns_forward.1 = (f32[1024,128]{1,0:T(8,128)S(1)}, f32[5,3,8,128]{3,2,1,0:T(8,128)S(1)}) custom-call(f32[1,128,1024]{2,1,0:T(8,128)} %guess_ref.1, f32[128,1024]{1,0:T(8,128)} %start_ref.1, f32[128,1024]{1,0:T(8,128)} %source_ref.1, bf16[8,128,128]{2,1,0:T(8,128)(2,1)} %constant.10.clone.high_ref.high_across_ref, ...), custom_call_target="tpu_custom_call" | custom-call | tf_op jit(solution)/shard_map/columns_forward/pallas_call | solution.py:262
  1.7 0.0 copy-start
  1.7 0.0 copy-start.1
  1.7 0.0 copy-start.2
  1.7 0.0 copy-start.3
  1.7 24.4 %all_to_all.10 = f32[128,8,128]{2,1,0:T(8,128)S(1)} all-to-all(f32[128,8,128]{2,1,0:T(8,128)S(1)} %bitcast.7), channel_id=1, replica_groups=mesh['z'=4,'y'=4,'x'=4,'core'=2] {'core','z','x','y'}, dimensions={0} | all-to-all | bytes 1048576 | tf_op jit(solution)/shard_map/all_to_all | solution.py:278
  26.1 0.0 copy-done
  26.1 0.0 copy-done.1
  26.1 0.0 copy-done.2
  26.1 0.0 copy-done.3
  26.1 0.7 %rows_and_time.1 = f32[2,4,4,4,8,128]{5,4,3,2,1,0:T(8,128)S(1)} custom-call(f32[2,4,4,4,8,128]{5,4,3,2,1,0:T(8,128)S(1)} %bitcast.5, f32[5,3,8,128]{3,2,1,0:T(8,128)S(1)} %get-tuple-element.8.symbols_ref, bf16[8,128,128]{2,1,0:T(8,128)(2,1)S(1)} %copy-done.3, bf16[8,128,128]{2,1,0:T(8,128)(2,1)S(1)} %copy-done.2, bf16[8,128,128]{2,1,0:T(8,128)(2,1)S(1)} %copy-done.1, ...), custom_call_target="tpu_custom_call" | custom-call | tf_op jit(solution)/shard_map/rows_and_time/pallas_call | solution.py:279
  26.8 17.5 %all_to_all.11 = f32[128,8,128]{2,1,0:T(8,128)S(1)} all-to-all(f32[128,8,128]{2,1,0:T(8,128)S(1)} %bitcast.6), channel_id=1, replica_groups=mesh['z'=4,'y'=4,'x'=4,'core'=2] {'core','z','x','y'}, dimensions={0} | all-to-all | bytes 1048576 | tf_op jit(solution)/shard_map/all_to_all | solution.py:289
  44.4 1.2 %columns_inverse.1 = f32[1,128,1024]{2,1,0:T(8,128)} custom-call(f32[1024,128]{1,0:T(8,128)S(1)} %bitcast.4, bf16[8,128,128]{2,1,0:T(8,128)(2,1)S(1)} %copy-done.1, bf16[8,128,128]{2,1,0:T(8,128)(2,1)S(1)} %copy-done), custom_call_target="tpu_custom_call" | custom-call | tf_op jit(solution)/shard_map/columns_inverse/pallas_call | solution.py:290
Async XLA Ops:
  1.7 24.4 %copy-start = (bf16[8,128,128]{2,1,0:T(8,128)(2,1)S(1)}, bf16[8,128,128]{2,1,0:T(8,128)(2,1)}, u32[]{:S(2)}) copy-start(bf16[8,128,128]{2,1,0:T(8,128)(2,1)} %constant.11.clone.low_ref.low_across_ref) | copy-start | bytes 786436
  1.7 24.4 %copy-start.1 = (bf16[8,128,128]{2,1,0:T(8,128)(2,1)S(1)}, bf16[8,128,128]{2,1,0:T(8,128)(2,1)}, u32[]{:S(2)}) copy-start(bf16[8,128,128]{2,1,0:T(8,128)(2,1)} %constant.10.clone.high_ref.high_across_ref) | copy-start | bytes 786436
  1.7 24.4 %copy-start.2 = (bf16[8,128,128]{2,1,0:T(8,128)(2,1)S(1)}, bf16[8,128,128]{2,1,0:T(8,128)(2,1)}, u32[]{:S(2)}) copy-start(bf16[8,128,128]{2,1,0:T(8,128)(2,1)} %constant.9.clone.low_ref) | copy-start | bytes 786436
  1.7 24.4 %copy-start.3 = (bf16[8,128,128]{2,1,0:T(8,128)(2,1)S(1)}, bf16[8,128,128]{2,1,0:T(8,128)(2,1)}, u32[]{:S(2)}) copy-start(bf16[8,128,128]{2,1,0:T(8,128)(2,1)} %constant.8.clone.high_ref) | copy-start | bytes 786436
